TPU v7x, 32 devices: a whole 2x2x4 slice. The times are simulated.
32 devices in a mesh: row: 4 (over y, core), col: 8 (over z, x).
Axes of the slice: x: 2, y: 2, z: 4, core: 2. Of those that a mesh axis runs over, the one named last changes fastest.
Arguments:
- phase: float32 [512, 32, 512], P('col', 'row'), may hold values from -6 to 6
- velocity: float32 [3, 512, 32, 512], P(None, 'col', 'row'), may hold values from -12 to 12
Outputs:
- phase_next: float32 [512, 32, 512], P('col', 'row')
- velocity_next: float32 [3, 512, 32, 512], P(None, 'col', 'row')
All inputs are finite; a program needn't handle non-finite values.
Results may differ from a plain program's by a relative error of at most 0.013.
Values may be sent and summed in bfloat16 or wider, within the bound.
A program may use at most 128 MiB of HBM per device.

v0:
```python
import math
import jax
import jax.numpy as jnp
from jax import lax
from jax.sharding import PartitionSpec as P

NX = 512
NY = 512
KC = 192
KY = 384
time_step = 0.001
epsilon = 0.01
mobility = 1.0
reynolds = 100.0
stabilizer = 2.0


def cos_sin(row_index, col_index, period):
    residue = row_index[:, None] * col_index[None, :] % period
    angles = residue.astype(jnp.float32) * (2.0 * math.pi / period)
    return jnp.stack([jnp.cos(angles), jnp.sin(angles)]).astype(jnp.bfloat16)


def pair_sum(pieces, direction, stack_axis):
    if direction < 0:
        real_part = pieces[0, 0] + pieces[1, 1]
        imag_part = pieces[1, 0] - pieces[0, 1]
    else:
        real_part = pieces[0, 0] - pieces[1, 1]
        imag_part = pieces[0, 1] + pieces[1, 0]
    return jnp.stack([real_part, imag_part], axis=stack_axis)


def times_i(values):
    return jnp.stack([-values[:, 1], values[:, 0]], axis=1)


def phase_terms(phase, velocity, gradient, lap_field):
    advect = velocity[0] * gradient[0] + velocity[1] * gradient[1] + velocity[2] * gradient[2]
    bulk_term = phase * phase * phase - phase
    potential = bulk_term - epsilon * epsilon * lap_field
    return (advect, bulk_term, potential)


def momentum(velocity, vortex, gradient, potential):
    return jnp.stack(
        [
            velocity[1] * vortex[2] - velocity[2] * vortex[1] + potential * gradient[0],
            velocity[2] * vortex[0] - velocity[0] * vortex[2] + potential * gradient[1],
            velocity[0] * vortex[1] - velocity[1] * vortex[0] + potential * gradient[2],
        ]
    )


def on_device(phase, velocity):
    col_count = lax.axis_size("col")
    row_count = lax.axis_size("row")
    rows_y = phase.shape[0]
    planes = phase.shape[1]
    total_z = planes * row_count
    half_z = 3 * total_z // 8
    modes_z = 2 * half_z
    kx_local = KC // col_count
    ky_local = KY // row_count
    scale_inv = 1.0 / (NX * NY * total_z)
    table_x = cos_sin(jnp.arange(NX, dtype=jnp.int32), jnp.arange(KC, dtype=jnp.int32), NX)
    table_y = cos_sin(jnp.arange(NY, dtype=jnp.int32), jnp.arange(KY, dtype=jnp.int32) - KC, NY)
    table_z = cos_sin(
        jnp.arange(total_z, dtype=jnp.int32), jnp.arange(modes_z, dtype=jnp.int32) - half_z, total_z
    )
    y_forward = table_y.reshape(2, col_count, rows_y, KY)
    y_inverse = table_y.reshape(2, col_count, rows_y, row_count, ky_local)
    z_table = table_z.reshape(2, row_count, planes, modes_z)
    weight = jnp.where(jnp.arange(KC) == 0, 1.0, 2.0).astype(jnp.bfloat16)[:, None, None, None]

    def along_y(incoming):
        field_count = incoming.shape[1]
        shaped = incoming.reshape(incoming.shape[0], field_count, col_count, 2, rows_y, planes)
        pieces = jnp.einsum(
            "afcpyz,tcyb->ptafbz", shaped, y_forward, preferred_element_type=jnp.float32
        )
        joined = pair_sum(pieces, -1, 2).astype(jnp.bfloat16)
        return joined.reshape(incoming.shape[0], field_count, 2, KY * planes)

    def along_z(incoming):
        field_count = incoming.shape[1]
        shaped = incoming.reshape(incoming.shape[0], field_count, 2, row_count, ky_local, planes)
        pieces = jnp.einsum(
            "afprbz,trzm->ptafbm", shaped, z_table, preferred_element_type=jnp.float32
        )
        joined = pair_sum(pieces, -1, 2) * scale_inv
        return joined.reshape(incoming.shape[0], field_count, 2, ky_local * modes_z)

    def back_y(incoming):
        field_count = incoming.shape[1]
        shaped = incoming.reshape(incoming.shape[0], field_count, 2, row_count, planes, ky_local)
        pieces = jnp.einsum(
            "afprzb,tcyrb->ptafcyz", shaped, y_inverse, preferred_element_type=jnp.float32
        )
        joined = pair_sum(pieces, 1, 3).astype(jnp.bfloat16)
        return joined.reshape(incoming.shape[0], field_count, col_count * 2 * rows_y * planes)

    def back_x(incoming):
        field_count = incoming.shape[1]
        shaped = incoming.reshape(KC, field_count, 2, rows_y, planes)
        scaled = jnp.stack([shaped[:, :, 0] * weight, -(shaped[:, :, 1] * weight)], axis=2)
        return jnp.einsum("afpyz,pxa->fyzx", scaled, table_x, preferred_element_type=jnp.float32)

    def forward(fields):
        field_count = fields.shape[0]
        pieces = jnp.einsum(
            "fyzx,txa->tafyz",
            fields.astype(jnp.bfloat16),
            table_x,
            preferred_element_type=jnp.float32,
        )
        x_lines = jnp.stack([pieces[0], -pieces[1]], axis=2).astype(jnp.bfloat16)
        x_lines = x_lines.reshape(KC, field_count, 2 * rows_y * planes)
        spread = along_y(lax.all_to_all(x_lines, "col", split_axis=0, concat_axis=2, tiled=True))
        return along_z(lax.all_to_all(spread, "row", split_axis=3, concat_axis=3, tiled=True))

    def inverse(spectra):
        field_count = spectra.shape[1]
        shaped = spectra.astype(jnp.bfloat16).reshape(kx_local, field_count, 2, ky_local, modes_z)
        pieces = jnp.einsum(
            "afpbm,trzm->ptafrzb", shaped, z_table, preferred_element_type=jnp.float32
        )
        z_planes = (
            pair_sum(pieces, 1, 2)
            .astype(jnp.bfloat16)
            .reshape(kx_local, field_count, 2, total_z * ky_local)
        )
        spread = back_y(lax.all_to_all(z_planes, "row", split_axis=3, concat_axis=3, tiled=True))
        return back_x(lax.all_to_all(spread, "col", split_axis=2, concat_axis=0, tiled=True))

    spectra = forward(jnp.concatenate([phase[None], velocity], axis=0))
    wave_x = (lax.axis_index("col") * kx_local + jnp.arange(kx_local, dtype=jnp.int32)).astype(
        jnp.float32
    )[:, None, None]
    modes_y = lax.axis_index("row") * ky_local + jnp.arange(ky_local, dtype=jnp.int32) - KC
    wave_y = jnp.broadcast_to(modes_y.astype(jnp.float32)[:, None], (ky_local, modes_z)).reshape(-1)
    z_values = (jnp.arange(modes_z, dtype=jnp.int32) - half_z).astype(jnp.float32) * (NX / total_z)
    wave_z = jnp.broadcast_to(z_values[None, :], (ky_local, modes_z)).reshape(-1)
    squared = wave_x * wave_x + wave_y * wave_y + wave_z * wave_z
    coeff_phase = spectra[:, 0]
    coeff_u = spectra[:, 1]
    coeff_v = spectra[:, 2]
    coeff_w = spectra[:, 3]
    gradients = [
        times_i(wave_x * coeff_phase),
        times_i(wave_y * coeff_phase),
        times_i(wave_z * coeff_phase),
    ]
    laplace = -squared * coeff_phase
    vortex_hat = [
        times_i(wave_y * coeff_w - wave_z * coeff_v),
        times_i(wave_z * coeff_u - wave_x * coeff_w),
        times_i(wave_x * coeff_v - wave_y * coeff_u),
    ]
    leading = inverse(jnp.stack(gradients + [laplace], axis=1))
    advect, bulk_term, potential = phase_terms(phase, velocity, leading[0:3], leading[3])
    phase_side = forward(jnp.stack([advect, bulk_term]))
    vortex = inverse(jnp.stack(vortex_hat, axis=1))
    flow_side = forward(momentum(velocity, vortex, leading[0:3], potential))
    nonlinear = jnp.concatenate([phase_side, flow_side], axis=1)
    mean_mode = (wave_x == 0) & (wave_y == 0) & (wave_z == 0)
    advect_hat = jnp.where(mean_mode, 0.0, nonlinear[:, 0])
    bulk_hat = nonlinear[:, 1]
    stable_part = 1.0 / time_step + mobility * stabilizer * squared
    new_phase = (stable_part * coeff_phase - advect_hat - mobility * squared * bulk_hat) / (
        stable_part + mobility * epsilon * epsilon * squared * squared
    )
    viscous = 1.0 / time_step + squared / reynolds
    unprojected = [
        (spectra[:, 1 + j] / time_step + nonlinear[:, 2 + j]) / viscous for j in range(3)
    ]
    normal_part = (
        wave_x * unprojected[0] + wave_y * unprojected[1] + wave_z * unprojected[2]
    ) / jnp.maximum(squared, 1.0)
    waves = [wave_x, wave_y, wave_z]
    new_flow = [unprojected[j] - waves[j] * normal_part for j in range(3)]
    result = inverse(jnp.stack([new_phase] + new_flow, axis=1))
    return (result[0], result[1:4])


def solution(mesh):
    return jax.shard_map(
        on_device,
        mesh=mesh,
        in_specs=(P("col", "row", None), P(None, "col", "row", None)),
        out_specs=(P("col", "row", None), P(None, "col", "row", None)),
        check_vma=False,
    )
```

profile of v0, /device:TPU:0, one launch (start us, length us, event | category | flops | bytes accessed | tf_op | source)
XLA Modules:
  0.0 845.1 jit_solution(9600123166907076406)
XLA Ops:
  13.6 7.5 all-to-all-start
  21.4 4.2 cosine_convert_fusion.1
  25.6 5.6 cosine_convert_fusion
  31.2 26.8 %all-to-all-done = bf16[192,4,1024]{2,1,0:T(4,128)(2,1)S(1)} async-done(((bf16[192,4,1024]{2,1,0:T(4,128)(2,1)}), bf16[192,4,1024]{2,1,0:T(4,128)(2,1)S(1)}, u32[]{:S(2)}, u32[]{:S(2)}) %all-to-all-start) | async-done | bytes 1572896 | tf_op jit(solution)/shard_map/all_to_all | solution.py:119
  58.5 5.9 copy.377
  64.4 8.6 %copy.378 = bf16[24,4,8,2,64,8]{4,0,2,5,3,1:T(8,128)(2,1)S(1)} copy(bf16[24,4,8,2,64,8]{0,5,4,3,2,1:T(8,128)(2,1)} %bitcast.525) | data formatting | bytes 3145728 | tf_op jit(solution)/shard_map/reshape | solution.py:78
  87.2 25.2 %copy.564 = bf16[24,4,2,3072]{0,1,2,3:T(4,128)(2,1)} copy(bf16[24,4,2,3072]{0,3,1,2:T(8,128)(2,1)S(1)} %pad_maximum_fusion) | data formatting | bytes 2359296 | tf_op jit(solution)/shard_map/stack | solution.py:31
  112.4 10.7 %reshape.1359 = bf16[4,2,73728]{2,1,0:T(2,128)(2,1)} reshape(bf16[3072,2,4,24]{3,2,1,0:T(4,128)(2,1)} %bitcast.532) | data formatting | bytes 2359296
  128.0 14.4 %all-to-all-done.1 = bf16[4,2,73728]{2,1,0:T(2,128)(2,1)S(1)} async-done(((bf16[4,2,73728]{2,1,0:T(2,128)(2,1)}), bf16[4,2,73728]{2,1,0:T(2,128)(2,1)S(1)}, u32[]{:S(2)}, u32[]{:S(2)}) %all-to-all-start.1) | async-done | bytes 1179680 | tf_op jit(solution)/shard_map/all_to_all | solution.py:120
  142.4 10.2 %reshape.1360 = bf16[3072,2,4,24]{3,2,1,0:T(4,128)(2,1)} reshape(bf16[4,2,73728]{2,1,0:T(2,128)(2,1)S(1)} %all-to-all-done.1) | data formatting | bytes 2359296
  152.6 9.8 %copy.383 = bf16[24,4,2,4,96,8]{4,5,3,2,1,0:T(8,128)(2,1)S(1)} copy(bf16[24,4,2,4,96,8]{0,1,2,5,4,3:T(4,128)(2,1)} %bitcast.538) | data formatting | bytes 2359296 | tf_op jit(solution)/shard_map/reshape | solution.py:87
  166.6 4.2 add.442
  173.8 4.4 sub.259
  200.0 8.0 copy.424
  208.0 8.0 reshape.1365
  223.7 6.5 copy.393
  230.2 10.3 %reshape.1361 = bf16[4,2,73728]{2,1,0:T(2,128)(2,1)} reshape(bf16[3072,2,4,24]{3,2,1,0:T(4,128)(2,1)} %bitcast.533) | data formatting | bytes 2359296
  240.5 4.0 all-to-all-start.2
  244.5 7.8 reshape.1366
  252.3 5.3 fusion.12
  258.8 5.1 copy.429
  263.9 10.5 %copy.562 = bf16[24,3,8192]{0,1,2:T(4,128)(2,1)} copy(bf16[24,3,8192]{0,2,1:T(8,128)(2,1)} %bitcast.534) | data formatting | bytes 2359296 | tf_op jit(solution)/shard_map/convert_element_type | solution.py:100
  274.4 10.9 %reshape.1367 = bf16[8,2,36864]{2,1,0:T(2,128)(2,1)} reshape(bf16[8192,3,24]{2,1,0:T(4,128)(2,1)} %bitcast.521) | data formatting | bytes 2359296
  285.3 4.4 all-to-all-start.7
  289.8 10.2 %reshape.1362 = bf16[3072,2,4,24]{3,2,1,0:T(4,128)(2,1)} reshape(bf16[4,2,73728]{2,1,0:T(2,128)(2,1)S(1)} %all-to-all-done.2) | data formatting | bytes 2359296
  300.0 7.1 fusion.6
  308.9 6.6 copy.398
  315.5 12.2 %copy.563 = bf16[24,4,8192]{0,1,2:T(4,128)(2,1)} copy(bf16[24,4,8192]{0,2,1:T(8,128)(2,1)} %bitcast.526) | data formatting | bytes 3145728 | tf_op jit(solution)/shard_map/convert_element_type | solution.py:100
  327.7 12.6 %reshape.1363 = bf16[8,2,49152]{2,1,0:T(2,128)(2,1)} reshape(bf16[8192,4,24]{2,1,0:T(4,128)(2,1)} %bitcast.527) | data formatting | bytes 3145728
  340.4 6.2 all-to-all-start.3
  346.6 11.4 %reshape.1368 = bf16[8192,3,24]{2,1,0:T(4,128)(2,1)} reshape(bf16[8,2,36864]{2,1,0:T(2,128)(2,1)} %all-to-all-done.7) | data formatting | bytes 2359296
  358.0 11.2 %copy.559 = bf16[24,3,8,1024]{0,2,3,1:T(8,128)(2,1)} copy(bf16[24,3,8,1024]{0,1,3,2:T(4,128)(2,1)} %bitcast.522) | data formatting | bytes 2359296 | tf_op jit(solution)/shard_map/all_to_all | solution.py:134
  369.2 7.4 reshape.1323
  383.9 13.1 %reshape.1364 = bf16[8192,4,24]{2,1,0:T(4,128)(2,1)} reshape(bf16[8,2,49152]{2,1,0:T(2,128)(2,1)S(1)} %all-to-all-done.3) | data formatting | bytes 3145728
  397.0 12.1 %copy.558 = bf16[24,4,8,1024]{0,2,3,1:T(8,128)(2,1)} copy(bf16[24,4,8,1024]{0,1,3,2:T(4,128)(2,1)} %bitcast.528) | data formatting | bytes 3145728 | tf_op jit(solution)/shard_map/all_to_all | solution.py:134
  409.1 10.1 %reshape.1319 = bf16[192,4,2,64,8]{0,4,3,2,1:T(8,128)(2,1)S(1)} reshape(bf16[8,24,4,1024]{1,0,3,2:T(8,128)(2,1)} %bitcast.523) | data formatting | bytes 3145728 | tf_op jit(solution)/shard_map/reshape | solution.py:105
  435.6 17.4 %all-to-all-done.4 = bf16[192,2,1024]{2,1,0:T(2,128)(2,1)S(1)} async-done(((bf16[192,2,1024]{2,1,0:T(2,128)(2,1)}), bf16[192,2,1024]{2,1,0:T(2,128)(2,1)S(1)}, u32[]{:S(2)}, u32[]{:S(2)}) %all-to-all-start.4) | async-done | bytes 786464 | tf_op jit(solution)/shard_map/all_to_all | solution.py:119
  456.4 4.7 copy.408
  464.9 19.1 %copy.566 = bf16[24,2,2,3072]{0,1,2,3:T(2,128)(2,1)S(1)} copy(bf16[24,2,2,3072]{0,3,1,2:T(8,128)(2,1)S(1)} %pad_maximum_fusion.3) | data formatting | bytes 1179648 | tf_op jit(solution)/shard_map/stack | solution.py:31
  484.0 4.7 reshape.1371
  501.6 4.5 all-to-all-start.8
  506.9 5.3 reshape.1372
  512.2 5.9 copy.413
  526.8 16.3 %all-to-all-done.8 = bf16[192,3,1024]{2,1,0:T(4,128)(2,1)} async-done(((bf16[192,3,1024]{2,1,0:T(4,128)(2,1)}), bf16[192,3,1024]{2,1,0:T(4,128)(2,1)}, u32[]{:S(2)}, u32[]{:S(2)}) %all-to-all-start.8) | async-done | bytes 1179680 | tf_op jit(solution)/shard_map/all_to_all | solution.py:119
  545.0 4.5 copy.439
  549.5 6.6 copy.440
  568.7 42.6 %copy.565 = bf16[24,3,2,3072]{0,2,1,3:T(2,128)(2,1)} copy(bf16[24,3,2,3072]{0,3,1,2:T(8,128)(2,1)S(1)} %pad_maximum_fusion.1) | data formatting | bytes 1769472 | tf_op jit(solution)/shard_map/stack | solution.py:31
  611.3 8.2 reshape.1369
  619.5 4.7 all-to-all-start.9
  629.0 7.9 all-to-all-done.9
  636.9 8.7 %reshape.1370 = bf16[3072,3,2,24]{3,2,1,0:T(2,128)(2,1)} reshape(bf16[4,2,55296]{2,1,0:T(2,128)(2,1)} %all-to-all-done.9) | data formatting | bytes 1769472
  645.6 9.0 %copy.445 = bf16[24,3,2,4,96,8]{4,5,3,2,1,0:T(8,128)(2,1)S(1)} copy(bf16[24,3,2,4,96,8]{0,2,1,5,4,3:T(2,128)(2,1)} %bitcast.540) | data formatting | bytes 1769472 | tf_op jit(solution)/shard_map/reshape | solution.py:87
  680.0 6.5 copy.455
  686.5 9.7 %reshape.1373 = bf16[4,2,73728]{2,1,0:T(2,128)(2,1)S(1)} reshape(bf16[3072,2,4,24]{3,2,1,0:T(4,128)(2,1)} %bitcast.537) | data formatting | bytes 2359296
  696.2 18.3 %all_to_all.120 = bf16[4,2,73728]{2,1,0:T(2,128)(2,1)S(1)} all-to-all(bf16[4,2,73728]{2,1,0:T(2,128)(2,1)S(1)} %reshape.1373), channel_id=1, replica_groups=mesh['row'=4,'col'=8] {'row'}, dimensions={0} | all-to-all | bytes 2359296 | tf_op jit(solution)/shard_map/all_to_all | solution.py:133
  714.5 10.2 %reshape.1374 = bf16[3072,2,4,24]{3,2,1,0:T(4,128)(2,1)} reshape(bf16[4,2,73728]{2,1,0:T(2,128)(2,1)S(1)} %all_to_all.120) | data formatting | bytes 2359296
  724.7 7.1 fusion.9
  733.6 6.7 copy.460
  740.3 12.2 %copy.561 = bf16[24,4,8192]{0,1,2:T(4,128)(2,1)} copy(bf16[24,4,8192]{0,2,1:T(8,128)(2,1)} %bitcast.529) | data formatting | bytes 3145728 | tf_op jit(solution)/shard_map/convert_element_type | solution.py:100
  752.4 11.9 %reshape.1375 = bf16[8,2,49152]{2,1,0:T(2,128)(2,1)S(1)} reshape(bf16[8192,4,24]{2,1,0:T(4,128)(2,1)} %bitcast.530) | data formatting | bytes 3145728
  764.4 40.3 %all_to_all.121 = bf16[8,2,49152]{2,1,0:T(2,128)(2,1)S(1)} all-to-all(bf16[8,2,49152]{2,1,0:T(2,128)(2,1)S(1)} %reshape.1375), channel_id=1, replica_groups=mesh['row'=4,'col'=8] {'col'}, dimensions={0} | all-to-all | bytes 3145728 | tf_op jit(solution)/shard_map/all_to_all | solution.py:134
  804.7 12.9 %reshape.1376 = bf16[8192,4,24]{2,1,0:T(4,128)(2,1)} reshape(bf16[8,2,49152]{2,1,0:T(2,128)(2,1)S(1)} %all_to_all.121) | data formatting | bytes 3145728
  817.6 12.1 %copy.557 = bf16[24,4,8,1024]{0,2,3,1:T(8,128)(2,1)} copy(bf16[24,4,8,1024]{0,1,3,2:T(4,128)(2,1)} %bitcast.531) | data formatting | bytes 3145728 | tf_op jit(solution)/shard_map/all_to_all | solution.py:134
  829.7 9.6 %reshape.1327 = bf16[192,4,2,64,8]{0,4,3,2,1:T(8,128)(2,1)S(1)} reshape(bf16[8,24,4,1024]{1,0,3,2:T(8,128)(2,1)} %bitcast.524) | data formatting | bytes 3145728 | tf_op jit(solution)/shard_map/reshape | solution.py:105
  (256 shorter events, 176.3 us)
Async XLA Ops:
  2.3 5.5 copy-start.4
  2.3 5.5 copy-start.7
  13.6 44.5 %all-to-all-start = ((bf16[192,4,1024]{2,1,0:T(4,128)(2,1)}), bf16[192,4,1024]{2,1,0:T(4,128)(2,1)S(1)}, u32[]{:S(2)}, u32[]{:S(2)}) async-start(bf16[192,4,1024]{2,1,0:T(4,128)(2,1)} %copy.375), calls=%async_computation | async-start | bytes 3145728 | tf_op jit(solution)/shard_map/all_to_all | solution.py:119
  21.3 198.4 %copy-start.27 = (bf16[1,4,8,24]{3,2,1,0:T(8,128)(2,1)}, bf16[1,4,8,24]{3,2,1,0:T(8,128)(2,1)S(1)}, u32[]{:S(2)}) copy-start(bf16[1,4,8,24]{3,2,1,0:T(8,128)(2,1)S(1)} %get-tuple-element.50) | copy-start | bytes 4612
  21.3 198.4 %copy-start.31 = (bf16[1,4,8,24]{3,2,1,0:T(8,128)(2,1)}, bf16[1,4,8,24]{3,2,1,0:T(8,128)(2,1)S(1)}, u32[]{:S(2)}) copy-start(bf16[1,4,8,24]{3,2,1,0:T(8,128)(2,1)S(1)} %get-tuple-element.51) | copy-start | bytes 4612
  123.1 19.3 %all-to-all-start.1 = ((bf16[4,2,73728]{2,1,0:T(2,128)(2,1)}), bf16[4,2,73728]{2,1,0:T(2,128)(2,1)S(1)}, u32[]{:S(2)}, u32[]{:S(2)}) async-start(bf16[4,2,73728]{2,1,0:T(2,128)(2,1)} %reshape.1359), calls=%async_computation.1 | async-start | bytes 2359296 | tf_op jit(solution)/shard_map/all_to_all | solution.py:120
  126.6 51.7 %copy-start.38 = (f32[24]{0:T(128)}, f32[24]{0:T(128)S(1)}, u32[]{:S(2)}) copy-start(f32[24]{0:T(128)S(1)} %add_convert_fusion.2) | copy-start | bytes 292
  126.9 51.4 %copy-start.18 = (f32[2304]{0:T(1024)}, f32[2304]{0:T(1024)S(1)}, u32[]{:S(2)}) copy-start(f32[2304]{0:T(1024)S(1)} %reshape.1314) | copy-start | bytes 27652
  178.3 1.5 copy-start.1
  215.9 24.5 %all-to-all-start.6 = ((bf16[4,2,55296]{2,1,0:T(2,128)(2,1)}), bf16[4,2,55296]{2,1,0:T(2,128)(2,1)S(1)}, u32[]{:S(2)}, u32[]{:S(2)}) async-start(bf16[4,2,55296]{2,1,0:T(2,128)(2,1)} %reshape.1365), calls=%async_computation.6 | async-start | bytes 1769472 | tf_op jit(solution)/shard_map/all_to_all | solution.py:133
  240.5 44.9 %all-to-all-start.2 = ((bf16[4,2,73728]{2,1,0:T(2,128)(2,1)}), bf16[4,2,73728]{2,1,0:T(2,128)(2,1)S(1)}, u32[]{:S(2)}, u32[]{:S(2)}) async-start(bf16[4,2,73728]{2,1,0:T(2,128)(2,1)} %reshape.1361), calls=%async_computation.2 | async-start | bytes 2359296 | tf_op jit(solution)/shard_map/all_to_all | solution.py:133
  244.5 7.8 copy-start.21
  244.5 7.8 copy-start.24
  285.3 55.0 %all-to-all-start.7 = ((bf16[8,2,36864]{2,1,0:T(2,128)(2,1)}), bf16[8,2,36864]{2,1,0:T(2,128)(2,1)}, u32[]{:S(2)}, u32[]{:S(2)}) async-start(bf16[8,2,36864]{2,1,0:T(2,128)(2,1)} %reshape.1367), calls=%async_computation.7 | async-start | bytes 2359296 | tf_op jit(solution)/shard_map/all_to_all | solution.py:134
  289.8 10.2 %copy-start.22 = (bf16[1,8,64,4,96]{4,2,3,1,0:T(8,128)(2,1)S(1)}, bf16[1,8,64,4,96]{4,2,3,1,0:T(8,128)(2,1)}, u32[]{:S(2)}) copy-start(bf16[1,8,64,4,96]{4,2,3,1,0:T(8,128)(2,1)} %get-tuple-element.46) | copy-start | bytes 1179652
  289.8 10.2 %copy-start.25 = (bf16[1,8,64,4,96]{4,2,3,1,0:T(8,128)(2,1)S(1)}, bf16[1,8,64,4,96]{4,2,3,1,0:T(8,128)(2,1)}, u32[]{:S(2)}) copy-start(bf16[1,8,64,4,96]{4,2,3,1,0:T(8,128)(2,1)} %get-tuple-element.47) | copy-start | bytes 1179652
  340.4 43.5 %all-to-all-start.3 = ((bf16[8,2,49152]{2,1,0:T(2,128)(2,1)}), bf16[8,2,49152]{2,1,0:T(2,128)(2,1)S(1)}, u32[]{:S(2)}, u32[]{:S(2)}) async-start(bf16[8,2,49152]{2,1,0:T(2,128)(2,1)} %reshape.1363), calls=%async_computation.3 | async-start | bytes 3145728 | tf_op jit(solution)/shard_map/all_to_all | solution.py:134
  376.6 0.9 copy-start.5
  376.6 1.0 copy-start.8
  419.3 1.9 copy-start
  421.2 1.2 copy-start.3
  421.2 2.2 copy-start.10
  428.9 24.2 %all-to-all-start.4 = ((bf16[192,2,1024]{2,1,0:T(2,128)(2,1)}), bf16[192,2,1024]{2,1,0:T(2,128)(2,1)S(1)}, u32[]{:S(2)}, u32[]{:S(2)}) async-start(bf16[192,2,1024]{2,1,0:T(2,128)(2,1)} %copy.405), calls=%async_computation.4 | async-start | bytes 1572864 | tf_op jit(solution)/shard_map/all_to_all | solution.py:119
  456.4 4.7 copy-start.35
  456.4 4.7 copy-start.36
  488.7 13.0 %all-to-all-start.5 = ((bf16[4,2,36864]{2,1,0:T(2,128)(2,1)}), bf16[4,2,36864]{2,1,0:T(2,128)(2,1)S(1)}, u32[]{:S(2)}, u32[]{:S(2)}) async-start(bf16[4,2,36864]{2,1,0:T(2,128)(2,1)} %reshape.1371), calls=%async_computation.5 | async-start | bytes 1179648 | tf_op jit(solution)/shard_map/all_to_all | solution.py:120
  498.9 7.3 copy-start.19
  501.6 4.6 copy-start.11
  501.6 41.5 %all-to-all-start.8 = ((bf16[192,3,1024]{2,1,0:T(4,128)(2,1)}), bf16[192,3,1024]{2,1,0:T(4,128)(2,1)}, u32[]{:S(2)}, u32[]{:S(2)}) async-start(bf16[192,3,1024]{2,1,0:T(4,128)(2,1)} %copy.437), calls=%async_computation.8 | async-start | bytes 3145728 | tf_op jit(solution)/shard_map/all_to_all | solution.py:119
  512.2 5.9 copy-start.28
  512.2 5.9 copy-start.32
  611.3 12.9 %copy-start.2 = (f32[24,4,2,2304]{3,0,1,2:T(8,128)S(1)}, f32[24,4,2,2304]{3,0,1,2:T(8,128)}, u32[]{:S(2)}) copy-start(f32[24,4,2,2304]{3,0,1,2:T(8,128)} %copy-done.1) | copy-start | bytes 5308420
  611.3 12.9 %copy-start.14 = (f32[24,2304]{1,0:T(8,128)S(1)}, f32[24,2304]{1,0:T(8,128)}, u32[]{:S(2)}) copy-start(f32[24,2304]{1,0:T(8,128)} %get-tuple-element.40) | copy-start | bytes 663556
  611.3 12.9 %copy-start.15 = (f32[24,2304]{1,0:T(8,128)S(1)}, f32[24,2304]{1,0:T(8,128)}, u32[]{:S(2)}) copy-start(f32[24,2304]{1,0:T(8,128)} %get-tuple-element.42) | copy-start | bytes 663556
  611.3 12.9 %copy-start.16 = (f32[24,2304]{1,0:T(8,128)S(1)}, f32[24,2304]{1,0:T(8,128)}, u32[]{:S(2)}) copy-start(f32[24,2304]{1,0:T(8,128)} %get-tuple-element.45) | copy-start | bytes 663556
  611.3 12.9 %copy-start.37 = (pred[24,2304]{1,0:T(8,128)(4,1)S(1)}, pred[24,2304]{1,0:T(8,128)(4,1)}, u32[]{:S(2)}) copy-start(pred[24,2304]{1,0:T(8,128)(4,1)} %and_and_fusion) | copy-start | bytes 165892
  619.5 17.4 %all-to-all-start.9 = ((bf16[4,2,55296]{2,1,0:T(2,128)(2,1)}), bf16[4,2,55296]{2,1,0:T(2,128)(2,1)}, u32[]{:S(2)}, u32[]{:S(2)}) async-start(bf16[4,2,55296]{2,1,0:T(2,128)(2,1)} %reshape.1369), calls=%async_computation.9 | async-start | bytes 1769472 | tf_op jit(solution)/shard_map/all_to_all | solution.py:120
  645.6 9.0 %copy-start.29 = (bf16[1,4,8,24]{3,2,1,0:T(8,128)(2,1)S(1)}, bf16[1,4,8,24]{3,2,1,0:T(8,128)(2,1)}, u32[]{:S(2)}) copy-start(bf16[1,4,8,24]{3,2,1,0:T(8,128)(2,1)} %copy-done.27) | copy-start | bytes 4612
  645.6 9.0 %copy-start.33 = (bf16[1,4,8,24]{3,2,1,0:T(8,128)(2,1)S(1)}, bf16[1,4,8,24]{3,2,1,0:T(8,128)(2,1)}, u32[]{:S(2)}) copy-start(bf16[1,4,8,24]{3,2,1,0:T(8,128)(2,1)} %copy-done.31) | copy-start | bytes 4612
  667.6 0.9 copy-start.12
  667.6 1.0 copy-start.17
  667.6 1.0 copy-start.20
  667.6 1.0 copy-start.39
  673.3 2.7 copy-start.13
  673.3 2.7 copy-start.30
  673.3 2.7 copy-start.34
  714.5 10.2 %copy-start.23 = (bf16[1,8,64,4,96]{4,2,3,1,0:T(8,128)(2,1)S(1)}, bf16[1,8,64,4,96]{4,2,3,1,0:T(8,128)(2,1)}, u32[]{:S(2)}) copy-start(bf16[1,8,64,4,96]{4,2,3,1,0:T(8,128)(2,1)} %get-tuple-element.46) | copy-start | bytes 1179652
  714.5 10.2 %copy-start.26 = (bf16[1,8,64,4,96]{4,2,3,1,0:T(8,128)(2,1)S(1)}, bf16[1,8,64,4,96]{4,2,3,1,0:T(8,128)(2,1)}, u32[]{:S(2)}) copy-start(bf16[1,8,64,4,96]{4,2,3,1,0:T(8,128)(2,1)} %get-tuple-element.47) | copy-start | bytes 1179652
  839.3 0.9 copy-start.6
  839.3 1.0 copy-start.9
where the time goes:
time: 853 us; the launch traced here: 845 us
  local copies, waits for them, and re-layouts  566 us (66%)
  waiting for transfers between devices  89.2 us (10%)
  blocking collectives  58.6 us (7%)
  starting transfers between devices  46 us (5%)
  matrix products  41.3 us (5%)
  other arithmetic  40.8 us (5%)
    unnamed x100, local copies, waits for them, and re-layouts  187 us
    another operation x9, local copies, waits for them, and re-layouts, pair_sum(): return jnp.stack([real_part, imag_part], axis=stack_axis)  126 us
    all_to_all x3, waiting for transfers between devices, forward(): lax.all_to_all(x_lines, 'col', split_axis=0, concat_axis=2, tiled=True)  60.6 us
    all_to_all x1, blocking collectives, inverse(): lax.all_to_all(spread, 'col', split_axis=2, concat_axis=0, tiled=True)  40.3 us
    all_to_all x3, local copies, waits for them, and re-layouts, inverse(): lax.all_to_all(spread, 'col', split_axis=2, concat_axis=0, tiled=True)  35.3 us
    convert_element_type x3, local copies, waits for them, and re-layouts, back_y(): joined = pair_sum(pieces, 1, 3).astype(jnp.bfloat16)  34.9 us
    reshape x3, local copies, waits for them, and re-layouts, back_x(): shaped = incoming.reshape(KC, field_count, 2, rows_y, planes)  27.1 us
    all_to_all x3, waiting for transfers between devices, forward(): lax.all_to_all(spread, 'row', split_axis=3, concat_axis=3, tiled=True)  25.1 us
  transfers between devices with their start and end apart: 10, of which 7 were waited for; matrix products, arithmetic and copies ran while one was open for 23% of the time, Pallas kernels for 0%

commit v1 on v0

--- a/solution.py
+++ b/solution.py
@@ -131,7 +131,16 @@
             .reshape(kx_local, field_count, 2, total_z * ky_local)
         )
         spread = back_y(lax.all_to_all(z_planes, "row", split_axis=3, concat_axis=3, tiled=True))
-        return back_x(lax.all_to_all(spread, "col", split_axis=2, concat_axis=0, tiled=True))
+
+        def attach_bars_all(chunk, shard_axis):
+            return jnp.concatenate(
+                lax.all_to_all(
+                    jnp.stack(jnp.split(chunk, lax.axis_size(shard_axis), axis=2)), shard_axis, 0, 0
+                ),
+                axis=0,
+            )
+
+        return back_x(attach_bars_all(spread, "col"))
 
     spectra = forward(jnp.concatenate([phase[None], velocity], axis=0))
     wave_x = (lax.axis_index("col") * kx_local + jnp.arange(kx_local, dtype=jnp.int32)).astype(

time: 853 us -> 815 us (0.955)
  local copies, waits for them, and re-layouts: 566 us -> 514 us
  waiting for transfers between devices: 89.2 us -> 104 us
    another operation x12 -> x45, local copies, waits for them, and re-layouts: 16.3 us -> 94.6 us  [the longest x30 51.7 us: attach_bars_all(): jnp.stack(jnp.split(chunk, lax.axis_size(shard_axis), axis=2))]
    unnamed x100 -> x139, local copies, waits for them, and re-layouts: 187 us -> 130 us
    convert_element_type x3 -> x0, local copies, waits for them, and re-layouts: 34.9 us -> none  [back_y(): joined = pair_sum(pieces, 1, 3).astype(jnp.bfloat16)]
    reshape x3 -> x0, local copies, waits for them, and re-layouts: 27.1 us -> none  [back_x(): shaped = incoming.reshape(KC, field_count, 2, rows_y, planes)]
    all_to_all x2, waiting for transfers between devices: 3.51 us -> 18.7 us  [attach_bars_all(): lax.all_to_all(jnp.stack(jnp.split(chunk, lax.axis_size(shard_axis), axis...]
    all_to_all x3, local copies, waits for them, and re-layouts: 35.3 us -> 22.6 us  [attach_bars_all(): lax.all_to_all(jnp.stack(jnp.split(chunk, lax.axis_size(shard_axis), axis...]
  transfers between devices with their start and end apart: 10 -> 10, of which waited for: 7 -> 7; matrix products, arithmetic and copies ran while one was open for 23% -> 22% of each run, Pallas kernels for 0% -> 0%
where the time goes in v1:
time: 815 us; the launch traced here: 807 us
  local copies, waits for them, and re-layouts  514 us (63%)
  waiting for transfers between devices  104 us (13%)
  blocking collectives  59 us (7%)
  starting transfers between devices  45.8 us (6%)
  matrix products  41.4 us (5%)
  other arithmetic  39.7 us (5%)
    unnamed x139, local copies, waits for them, and re-layouts  130 us
    another operation x9, local copies, waits for them, and re-layouts, pair_sum(): return jnp.stack([real_part, imag_part], axis=stack_axis)  126 us
    all_to_all x3, waiting for transfers between devices, forward(): lax.all_to_all(x_lines, 'col', split_axis=0, concat_axis=2, tiled=True)  60.6 us
    another operation x30, local copies, waits for them, and re-layouts, attach_bars_all(): jnp.stack(jnp.split(chunk, lax.axis_size(shard_axis), axis=2))  51.7 us
    all_to_all x1, blocking collectives, attach_bars_all(): lax.all_to_all(jnp.stack(jnp.split(chunk, lax.axis_size(shard_axis), axis...  40.7 us
    another operation x3, local copies, waits for them, and re-layouts, back_x(): shaped = incoming.reshape(KC, field_count, 2, rows_y, planes)  26.6 us
    all_to_all x3, waiting for transfers between devices, forward(): lax.all_to_all(spread, 'row', split_axis=3, concat_axis=3, tiled=True)  25.1 us
    reshape x3, local copies, waits for them, and re-layouts, along_z(): incoming.reshape(incoming.shape[0], field_count, 2, row_count, ky_local,...  24.7 us
  transfers between devices with their start and end apart: 10, of which 7 were waited for; matrix products, arithmetic and copies ran while one was open for 22% of the time, Pallas kernels for 0%

profile of v1, /device:TPU:0, one launch (start us, length us, event | category | flops | bytes accessed | tf_op | source)
XLA Modules:
  0.0 806.6 jit_solution(3480015780920626249)
XLA Ops:
  2.3 3.7 copy.603
  12.4 7.5 all-to-all-start
  20.1 4.2 cosine_convert_fusion.1
  24.4 5.7 cosine_convert_fusion
  30.0 26.8 %all-to-all-done = bf16[192,4,1024]{2,1,0:T(4,128)(2,1)S(1)} async-done(((bf16[192,4,1024]{2,1,0:T(4,128)(2,1)}), bf16[192,4,1024]{2,1,0:T(4,128)(2,1)S(1)}, u32[]{:S(2)}, u32[]{:S(2)}) %all-to-all-start) | async-done | bytes 1572896 | tf_op jit(solution)/shard_map/all_to_all | solution.py:119
  57.3 5.8 copy.415
  63.1 8.6 %copy.416 = bf16[24,4,8,2,64,8]{4,0,2,5,3,1:T(8,128)(2,1)S(1)} copy(bf16[24,4,8,2,64,8]{0,5,4,3,2,1:T(8,128)(2,1)} %bitcast.546) | data formatting | bytes 3145728 | tf_op jit(solution)/shard_map/reshape | solution.py:78
  78.6 4.0 copy.417
  85.9 25.2 %copy.608 = bf16[24,4,2,3072]{0,1,2,3:T(4,128)(2,1)} copy(bf16[24,4,2,3072]{0,3,1,2:T(8,128)(2,1)S(1)} %pad_maximum_fusion) | data formatting | bytes 2359296 | tf_op jit(solution)/shard_map/stack | solution.py:31
  111.1 10.5 %reshape.1344 = bf16[4,2,73728]{2,1,0:T(2,128)(2,1)} reshape(bf16[3072,2,4,24]{3,2,1,0:T(4,128)(2,1)} %bitcast.548) | data formatting | bytes 2359296
  126.5 14.3 %all-to-all-done.1 = bf16[4,2,73728]{2,1,0:T(2,128)(2,1)S(1)} async-done(((bf16[4,2,73728]{2,1,0:T(2,128)(2,1)}), bf16[4,2,73728]{2,1,0:T(2,128)(2,1)S(1)}, u32[]{:S(2)}, u32[]{:S(2)}) %all-to-all-start.1) | async-done | bytes 1179680 | tf_op jit(solution)/shard_map/all_to_all | solution.py:120
  140.9 10.2 %reshape.1345 = bf16[3072,2,4,24]{3,2,1,0:T(4,128)(2,1)} reshape(bf16[4,2,73728]{2,1,0:T(2,128)(2,1)S(1)} %all-to-all-done.1) | data formatting | bytes 2359296
  151.0 9.8 %copy.421 = bf16[24,4,2,4,96,8]{4,5,3,2,1,0:T(8,128)(2,1)S(1)} copy(bf16[24,4,2,4,96,8]{0,1,2,5,4,3:T(4,128)(2,1)} %bitcast.552) | data formatting | bytes 2359296 | tf_op jit(solution)/shard_map/reshape | solution.py:87
  165.0 4.2 sub.259
  172.2 4.6 add.442
  197.5 7.9 copy.469
  205.4 8.0 reshape.1348
  213.4 3.7 all-to-all-start.6
  221.1 6.5 copy.431
  227.6 10.3 %reshape.1346 = bf16[4,2,73728]{2,1,0:T(2,128)(2,1)} reshape(bf16[3072,2,4,24]{3,2,1,0:T(4,128)(2,1)} %bitcast.549) | data formatting | bytes 2359296
  237.9 3.8 all-to-all-start.2
  241.7 7.7 reshape.1349
  249.4 5.4 fusion.12
  256.0 5.0 copy.474
  261.0 4.8 slice_bitcast_fusion.29
  285.5 4.7 all-to-all-start.7
  290.3 10.2 %reshape.1347 = bf16[3072,2,4,24]{3,2,1,0:T(4,128)(2,1)} reshape(bf16[4,2,73728]{2,1,0:T(2,128)(2,1)S(1)} %all-to-all-done.2) | data formatting | bytes 2359296
  300.5 7.1 fusion.6
  309.4 6.6 copy.436
  316.0 5.6 slice_bitcast_fusion.19
  338.9 6.2 all-to-all-start.3
  345.1 7.4 copy.483
  352.5 7.4 reshape_reshape.10
  363.7 18.7 %all-to-all-done.3 = bf16[8,24,4,1024]{3,1,2,0:T(8,128)(2,1)S(1)} async-done(((bf16[8,24,4,1024]{3,1,2,0:T(8,128)(2,1)}), bf16[8,24,4,1024]{3,1,2,0:T(8,128)(2,1)S(1)}, u32[]{:S(2)}, u32[]{:S(2)}) %all-to-all-start.3) | async-done | bytes 1572896 | tf_op jit(solution)/shard_map/all_to_all | solution.py:137
  382.4 7.6 copy.445
  390.0 9.6 %reshape_reshape.9 = bf16[192,4,2,64,8]{0,4,3,2,1:T(8,128)(2,1)S(1)} reshape(bf16[8,24,4,1024]{1,0,3,2:T(8,128)(2,1)} %copy.445) | data formatting | bytes 3145728 | tf_op jit(solution)/shard_map/reshape;reshape | solution.py:105
  409.3 3.9 all-to-all-start.4
  416.1 17.4 %all-to-all-done.4 = bf16[192,2,1024]{2,1,0:T(2,128)(2,1)S(1)} async-done(((bf16[192,2,1024]{2,1,0:T(2,128)(2,1)}), bf16[192,2,1024]{2,1,0:T(2,128)(2,1)S(1)}, u32[]{:S(2)}, u32[]{:S(2)}) %all-to-all-start.4) | async-done | bytes 786464 | tf_op jit(solution)/shard_map/all_to_all | solution.py:119
  436.8 4.7 copy.453
  445.3 19.1 %copy.610 = bf16[24,2,2,3072]{0,1,2,3:T(2,128)(2,1)S(1)} copy(bf16[24,2,2,3072]{0,3,1,2:T(8,128)(2,1)S(1)} %pad_maximum_fusion.3) | data formatting | bytes 1179648 | tf_op jit(solution)/shard_map/stack | solution.py:31
  464.4 4.7 reshape.1352
  482.1 4.6 all-to-all-start.8
  487.4 5.3 reshape.1353
  492.7 5.9 copy.458
  507.3 16.3 %all-to-all-done.8 = bf16[192,3,1024]{2,1,0:T(4,128)(2,1)} async-done(((bf16[192,3,1024]{2,1,0:T(4,128)(2,1)}), bf16[192,3,1024]{2,1,0:T(4,128)(2,1)}, u32[]{:S(2)}, u32[]{:S(2)}) %all-to-all-start.8) | async-done | bytes 1179680 | tf_op jit(solution)/shard_map/all_to_all | solution.py:119
  525.5 4.4 copy.490
  529.9 6.6 copy.491
  549.2 42.8 %copy.609 = bf16[24,3,2,3072]{0,2,1,3:T(2,128)(2,1)} copy(bf16[24,3,2,3072]{0,3,1,2:T(8,128)(2,1)S(1)} %pad_maximum_fusion.1) | data formatting | bytes 1769472 | tf_op jit(solution)/shard_map/stack | solution.py:31
  591.9 8.1 reshape.1350
  600.0 4.5 all-to-all-start.9
  609.3 7.9 all-to-all-done.9
  617.3 8.7 %reshape.1351 = bf16[3072,3,2,24]{3,2,1,0:T(2,128)(2,1)} reshape(bf16[4,2,55296]{2,1,0:T(2,128)(2,1)} %all-to-all-done.9) | data formatting | bytes 1769472
  625.9 9.0 %copy.496 = bf16[24,3,2,4,96,8]{4,5,3,2,1,0:T(8,128)(2,1)S(1)} copy(bf16[24,3,2,4,96,8]{0,2,1,5,4,3:T(2,128)(2,1)} %bitcast.554) | data formatting | bytes 1769472 | tf_op jit(solution)/shard_map/reshape | solution.py:87
  644.2 3.8 add.464
  660.4 6.5 copy.506
  666.9 9.8 %reshape.1354 = bf16[4,2,73728]{2,1,0:T(2,128)(2,1)S(1)} reshape(bf16[3072,2,4,24]{3,2,1,0:T(4,128)(2,1)} %bitcast.551) | data formatting | bytes 2359296
  676.7 18.3 %all_to_all.90 = bf16[4,2,73728]{2,1,0:T(2,128)(2,1)S(1)} all-to-all(bf16[4,2,73728]{2,1,0:T(2,128)(2,1)S(1)} %reshape.1354), channel_id=1, replica_groups=mesh['row'=4,'col'=8] {'row'}, dimensions={0} | all-to-all | bytes 2359296 | tf_op jit(solution)/shard_map/all_to_all | solution.py:133
  694.9 10.2 %reshape.1355 = bf16[3072,2,4,24]{3,2,1,0:T(4,128)(2,1)} reshape(bf16[4,2,73728]{2,1,0:T(2,128)(2,1)S(1)} %all_to_all.90) | data formatting | bytes 2359296
  705.1 7.1 fusion.9
  714.0 6.6 copy.511
  720.6 5.6 slice_bitcast_fusion.9
  742.7 40.7 %all_to_all.91 = bf16[8,24,4,1024]{3,1,2,0:T(8,128)(2,1)S(1)} all-to-all(bf16[8,24,4,1024]{3,1,2,0:T(8,128)(2,1)} %constant_dynamic-update-slice_fusion.16), channel_id=1, replica_groups=mesh['row'=4,'col'=8] {'col'}, dimensions={0} | all-to-all | bytes 3145728 | tf_op jit(solution)/shard_map/all_to_all | solution.py:137
  783.4 7.6 copy.520
  791.0 9.6 %reshape_reshape.11 = bf16[192,4,2,64,8]{0,4,3,2,1:T(8,128)(2,1)S(1)} reshape(bf16[8,24,4,1024]{1,0,3,2:T(8,128)(2,1)} %copy.520) | data formatting | bytes 3145728 | tf_op jit(solution)/shard_map/reshape;reshape | solution.py:105
  (322 shorter events, 205.1 us)
Async XLA Ops:
  2.3 4.3 copy-start.5
  2.3 4.3 copy-start.8
  2.3 3.7 copy-start.3
  12.4 44.4 %all-to-all-start = ((bf16[192,4,1024]{2,1,0:T(4,128)(2,1)}), bf16[192,4,1024]{2,1,0:T(4,128)(2,1)S(1)}, u32[]{:S(2)}, u32[]{:S(2)}) async-start(bf16[192,4,1024]{2,1,0:T(4,128)(2,1)} %copy.413), calls=%async_computation | async-start | bytes 3145728 | tf_op jit(solution)/shard_map/all_to_all | solution.py:119
  19.9 157.0 %copy-start.50 = (f32[24]{0:T(128)}, f32[24]{0:T(128)S(1)}, u32[]{:S(2)}) copy-start(f32[24]{0:T(128)S(1)} %add_convert_fusion.2) | copy-start | bytes 292
  20.1 197.0 %copy-start.39 = (bf16[1,4,8,24]{3,2,1,0:T(8,128)(2,1)}, bf16[1,4,8,24]{3,2,1,0:T(8,128)(2,1)S(1)}, u32[]{:S(2)}) copy-start(bf16[1,4,8,24]{3,2,1,0:T(8,128)(2,1)S(1)} %get-tuple-element.74) | copy-start | bytes 4612
  20.1 197.0 %copy-start.43 = (bf16[1,4,8,24]{3,2,1,0:T(8,128)(2,1)}, bf16[1,4,8,24]{3,2,1,0:T(8,128)(2,1)S(1)}, u32[]{:S(2)}) copy-start(bf16[1,4,8,24]{3,2,1,0:T(8,128)(2,1)S(1)} %get-tuple-element.75) | copy-start | bytes 4612
  121.5 19.3 %all-to-all-start.1 = ((bf16[4,2,73728]{2,1,0:T(2,128)(2,1)}), bf16[4,2,73728]{2,1,0:T(2,128)(2,1)S(1)}, u32[]{:S(2)}, u32[]{:S(2)}) async-start(bf16[4,2,73728]{2,1,0:T(2,128)(2,1)} %reshape.1344), calls=%async_computation.1 | async-start | bytes 2359296 | tf_op jit(solution)/shard_map/all_to_all | solution.py:120
  125.4 51.6 %copy-start.26 = (f32[2304]{0:T(1024)}, f32[2304]{0:T(1024)S(1)}, u32[]{:S(2)}) copy-start(f32[2304]{0:T(1024)S(1)} %reshape.1302) | copy-start | bytes 27652
  177.0 1.2 copy-start.1
  189.8 2.4 copy-start.38
  213.4 24.5 %all-to-all-start.6 = ((bf16[4,2,55296]{2,1,0:T(2,128)(2,1)}), bf16[4,2,55296]{2,1,0:T(2,128)(2,1)S(1)}, u32[]{:S(2)}, u32[]{:S(2)}) async-start(bf16[4,2,55296]{2,1,0:T(2,128)(2,1)} %reshape.1348), calls=%async_computation.6 | async-start | bytes 1769472 | tf_op jit(solution)/shard_map/all_to_all | solution.py:133
  237.9 47.7 %all-to-all-start.2 = ((bf16[4,2,73728]{2,1,0:T(2,128)(2,1)}), bf16[4,2,73728]{2,1,0:T(2,128)(2,1)S(1)}, u32[]{:S(2)}, u32[]{:S(2)}) async-start(bf16[4,2,73728]{2,1,0:T(2,128)(2,1)} %reshape.1346), calls=%async_computation.2 | async-start | bytes 2359296 | tf_op jit(solution)/shard_map/all_to_all | solution.py:133
  241.7 7.8 copy-start.32
  241.7 7.8 copy-start.35
  276.9 5.3 copy-start.31
  276.9 6.0 copy-start.30
  276.9 6.6 copy-start.29
  285.5 53.3 %all-to-all-start.7 = ((bf16[8,24,3,1024]{3,1,2,0:T(8,128)(2,1)}), bf16[8,24,3,1024]{3,1,2,0:T(8,128)(2,1)}, u32[]{:S(2)}, u32[]{:S(2)}) async-start(bf16[8,24,3,1024]{3,1,2,0:T(8,128)(2,1)} %constant_dynamic-update-slice_fusion.8), calls=%async_computation.7 | async-start | bytes 2359296 | tf_op jit(solution)/shard_map/all_to_all | solution.py:137
  290.3 10.2 %copy-start.33 = (bf16[1,8,64,4,96]{4,2,3,1,0:T(8,128)(2,1)S(1)}, bf16[1,8,64,4,96]{4,2,3,1,0:T(8,128)(2,1)}, u32[]{:S(2)}) copy-start(bf16[1,8,64,4,96]{4,2,3,1,0:T(8,128)(2,1)} %get-tuple-element.70) | copy-start | bytes 1179652
  290.3 10.2 %copy-start.36 = (bf16[1,8,64,4,96]{4,2,3,1,0:T(8,128)(2,1)S(1)}, bf16[1,8,64,4,96]{4,2,3,1,0:T(8,128)(2,1)}, u32[]{:S(2)}) copy-start(bf16[1,8,64,4,96]{4,2,3,1,0:T(8,128)(2,1)} %get-tuple-element.71) | copy-start | bytes 1179652
  332.3 0.9 copy-start.21
  332.3 1.6 copy-start.22
  332.3 2.3 copy-start.20
  332.3 3.0 copy-start.19
  338.9 43.5 %all-to-all-start.3 = ((bf16[8,24,4,1024]{3,1,2,0:T(8,128)(2,1)}), bf16[8,24,4,1024]{3,1,2,0:T(8,128)(2,1)S(1)}, u32[]{:S(2)}, u32[]{:S(2)}) async-start(bf16[8,24,4,1024]{3,1,2,0:T(8,128)(2,1)} %constant_dynamic-update-slice_fusion), calls=%async_computation.3 | async-start | bytes 3145728 | tf_op jit(solution)/shard_map/all_to_all | solution.py:137
  359.9 0.9 copy-start.6
  359.9 1.0 copy-start.9
  399.7 1.9 copy-start
  401.6 1.2 copy-start.4
  401.6 2.2 copy-start.11
  409.3 24.2 %all-to-all-start.4 = ((bf16[192,2,1024]{2,1,0:T(2,128)(2,1)}), bf16[192,2,1024]{2,1,0:T(2,128)(2,1)S(1)}, u32[]{:S(2)}, u32[]{:S(2)}) async-start(bf16[192,2,1024]{2,1,0:T(2,128)(2,1)} %copy.450), calls=%async_computation.4 | async-start | bytes 1572864 | tf_op jit(solution)/shard_map/all_to_all | solution.py:119
  436.8 4.7 copy-start.47
  436.8 4.7 copy-start.48
  469.1 13.0 %all-to-all-start.5 = ((bf16[4,2,36864]{2,1,0:T(2,128)(2,1)}), bf16[4,2,36864]{2,1,0:T(2,128)(2,1)S(1)}, u32[]{:S(2)}, u32[]{:S(2)}) async-start(bf16[4,2,36864]{2,1,0:T(2,128)(2,1)} %reshape.1352), calls=%async_computation.5 | async-start | bytes 1179648 | tf_op jit(solution)/shard_map/all_to_all | solution.py:120
  479.3 7.4 copy-start.27
  482.1 4.6 copy-start.12
  482.1 41.5 %all-to-all-start.8 = ((bf16[192,3,1024]{2,1,0:T(4,128)(2,1)}), bf16[192,3,1024]{2,1,0:T(4,128)(2,1)}, u32[]{:S(2)}, u32[]{:S(2)}) async-start(bf16[192,3,1024]{2,1,0:T(4,128)(2,1)} %copy.488), calls=%async_computation.8 | async-start | bytes 3145728 | tf_op jit(solution)/shard_map/all_to_all | solution.py:119
  492.7 5.9 copy-start.40
  492.7 5.9 copy-start.44
  591.9 12.6 %copy-start.15 = (f32[24,2304]{1,0:T(8,128)S(1)}, f32[24,2304]{1,0:T(8,128)}, u32[]{:S(2)}) copy-start(f32[24,2304]{1,0:T(8,128)} %get-tuple-element.64) | copy-start | bytes 663556
  591.9 12.6 %copy-start.16 = (f32[24,2304]{1,0:T(8,128)S(1)}, f32[24,2304]{1,0:T(8,128)}, u32[]{:S(2)}) copy-start(f32[24,2304]{1,0:T(8,128)} %get-tuple-element.66) | copy-start | bytes 663556
  591.9 12.6 %copy-start.17 = (f32[24,2304]{1,0:T(8,128)S(1)}, f32[24,2304]{1,0:T(8,128)}, u32[]{:S(2)}) copy-start(f32[24,2304]{1,0:T(8,128)} %get-tuple-element.69) | copy-start | bytes 663556
  591.9 12.6 %copy-start.49 = (pred[24,2304]{1,0:T(8,128)(4,1)S(1)}, pred[24,2304]{1,0:T(8,128)(4,1)}, u32[]{:S(2)}) copy-start(pred[24,2304]{1,0:T(8,128)(4,1)} %and_and_fusion) | copy-start | bytes 165892
  600.0 4.6 copy-start.2
  600.0 17.3 %all-to-all-start.9 = ((bf16[4,2,55296]{2,1,0:T(2,128)(2,1)}), bf16[4,2,55296]{2,1,0:T(2,128)(2,1)}, u32[]{:S(2)}, u32[]{:S(2)}) async-start(bf16[4,2,55296]{2,1,0:T(2,128)(2,1)} %reshape.1350), calls=%async_computation.9 | async-start | bytes 1769472 | tf_op jit(solution)/shard_map/all_to_all | solution.py:120
  625.9 9.0 %copy-start.41 = (bf16[1,4,8,24]{3,2,1,0:T(8,128)(2,1)S(1)}, bf16[1,4,8,24]{3,2,1,0:T(8,128)(2,1)}, u32[]{:S(2)}) copy-start(bf16[1,4,8,24]{3,2,1,0:T(8,128)(2,1)} %copy-done.39) | copy-start | bytes 4612
  625.9 9.0 %copy-start.45 = (bf16[1,4,8,24]{3,2,1,0:T(8,128)(2,1)S(1)}, bf16[1,4,8,24]{3,2,1,0:T(8,128)(2,1)}, u32[]{:S(2)}) copy-start(bf16[1,4,8,24]{3,2,1,0:T(8,128)(2,1)} %copy-done.43) | copy-start | bytes 4612
  648.0 0.9 copy-start.13
  648.0 1.0 copy-start.18
  648.0 1.0 copy-start.28
  648.0 1.0 copy-start.51
  654.1 2.3 copy-start.14
  654.1 2.3 copy-start.42
  654.1 2.3 copy-start.46
  694.9 10.2 %copy-start.34 = (bf16[1,8,64,4,96]{4,2,3,1,0:T(8,128)(2,1)S(1)}, bf16[1,8,64,4,96]{4,2,3,1,0:T(8,128)(2,1)}, u32[]{:S(2)}) copy-start(bf16[1,8,64,4,96]{4,2,3,1,0:T(8,128)(2,1)} %get-tuple-element.70) | copy-start | bytes 1179652
  694.9 10.2 %copy-start.37 = (bf16[1,8,64,4,96]{4,2,3,1,0:T(8,128)(2,1)S(1)}, bf16[1,8,64,4,96]{4,2,3,1,0:T(8,128)(2,1)}, u32[]{:S(2)}) copy-start(bf16[1,8,64,4,96]{4,2,3,1,0:T(8,128)(2,1)} %get-tuple-element.71) | copy-start | bytes 1179652
  736.9 0.9 copy-start.24
  736.9 1.6 copy-start.25
  736.9 2.3 copy-start.23
  800.6 0.9 copy-start.7
  800.6 1.0 copy-start.10
